TPU v7x, 32 devices: a whole 2x2x4 slice. The times are simulated.
32 devices in a mesh: tok: 8 (over z, y), voc: 4 (over x, core).
Axes of the slice: x: 2, y: 2, z: 4, core: 2. Of those that a mesh axis runs over, the one named last changes fastest.
Arguments:
- hidden: bfloat16 [96, 4096], P(('tok', 'voc'))
- head_weight: bfloat16 [4096, 16032], P(None, ('tok', 'voc'))
- actions: int32 [96], P(('tok', 'voc')), may hold values from 0 to 16031
- old_logp: bfloat16 [96], P(('tok', 'voc')), may hold values from -80 to 1
- advantage: bfloat16 [96], P(('tok', 'voc')), may hold values from -4 to 4
- loss_mask: int32 [96], P(('tok', 'voc')), may hold values 0 or 1
Outputs:
- grad_weight: bfloat16 [4096, 16032], P(None, ('tok', 'voc'))
- grad_hidden: float32 [96, 4096], P(('tok', 'voc'))
All inputs are finite; a program needn't handle non-finite values. No bound on the sum of `loss_mask` on one device may be relied on, other than what follows from the above.
Results may differ from a plain program's by a relative error of at most 0.0047.
Values may be sent and summed in bfloat16 or wider, within the bound.
A program may use at most 128 MiB of HBM per device.

v0:
```python
import jax
import jax.numpy as jnp
from jax import lax
from jax.sharding import PartitionSpec as P


def per_device(hidden, head_weight, actions, old_logp, advantage, loss_mask):
    hidden_all, old_all, advant_all = (
        lax.all_gather(hidden, ("tok", "voc"), axis=0, tiled=True),
        lax.all_gather(old_logp, ("tok", "voc"), axis=0, tiled=True),
        lax.all_gather(advantage, ("tok", "voc"), axis=0, tiled=True),
    )
    action_all, mask_all = (
        lax.all_gather(actions, ("tok", "voc"), axis=0, tiled=True),
        lax.all_gather(loss_mask, ("tok", "voc"), axis=0, tiled=True),
    )
    width = head_weight.shape[1]
    logits = jnp.dot(hidden_all, head_weight, preferred_element_type=jnp.float32)
    first_col = lax.axis_index(("tok", "voc")) * width
    columns = first_col + lax.broadcasted_iota(jnp.int32, logits.shape, 1)
    matches = columns == action_all[:, None]
    target_part = jnp.sum(jnp.where(matches, logits, 0.0), axis=1)
    top = lax.pmax(jnp.max(logits, axis=1), ("tok", "voc"))
    shifted = jnp.exp(logits - top[:, None])
    sumexp, moment, target = lax.psum(
        (jnp.sum(shifted, axis=1), jnp.sum(shifted * logits, axis=1), target_part), ("tok", "voc")
    )
    lse = top + jnp.log(sumexp)
    mean_logit = moment / sumexp
    advant = advant_all.astype(jnp.float32)
    ratio = jnp.exp(target - lse - old_all.astype(jnp.float32))
    clipped = (advant > 0.0) & (ratio > 1.2) | (advant < 0.0) & (ratio < 0.8)
    active = jnp.where(clipped, 0.0, 1.0).astype(jnp.float32)
    weights = mask_all.astype(jnp.float32)
    policy = -advant * ratio * active * weights
    probability = jnp.exp(logits - lse[:, None])
    onehot = matches.astype(jnp.float32)
    dlogits = policy[:, None] * (onehot - probability) + 0.05 * weights[:, None] * probability * (
        logits - mean_logit[:, None]
    )
    dlogits = dlogits.astype(jnp.bfloat16)
    partial_rows = lax.psum_scatter(
        lax.dot_general(
            dlogits, head_weight, (((1,), (1,)), ((), ())), preferred_element_type=jnp.float32
        ),
        "tok",
        scatter_dimension=0,
        tiled=True,
    )
    grad_hidden = lax.psum_scatter(partial_rows, "voc", scatter_dimension=0, tiled=True)
    grad_weight = lax.dot_general(
        hidden_all, dlogits, (((0,), (0,)), ((), ())), preferred_element_type=jnp.float32
    ).astype(jnp.bfloat16)
    return (grad_weight, grad_hidden)


def solution(mesh):
    placed = (
        P(("tok", "voc"), None),
        P(None, ("tok", "voc")),
        P(("tok", "voc")),
        P(("tok", "voc")),
        P(("tok", "voc")),
        P(("tok", "voc")),
    )
    return jax.shard_map(
        per_device,
        mesh=mesh,
        in_specs=placed,
        out_specs=(P(None, ("tok", "voc")), P(("tok", "voc"), None)),
        check_vma=False,
    )
```

profile of v0, /device:TPU:0, one launch (start us, length us, event | category | flops | bytes accessed | tf_op | source)
XLA Modules:
  0.0 323.1 jit_solution(7266715647205631639)
XLA Ops:
  7.3 46.5 %all-gather = bf16[32,3,4096]{2,1,0:T(4,128)(2,1)S(1)} all-gather(bf16[1,3,4096]{2,1,0:T(4,128)(2,1)} %bitcast.11), channel_id=1, replica_groups=mesh['tok'=8,'voc'=4] {'tok','voc'}, dimensions={0}, use_global_device_ids=true | all-gather | bytes 811008 | tf_op jit(solution)/shard_map/all_gather | solution.py:9
  53.7 0.7 reshape.20
  54.4 3.6 %fusion.12 = (f32[96]{0:T(128)S(1)}, f32[96,501]{1,0:T(8,128)S(1)}) fusion(bf16[96,4096]{1,0:T(8,128)(2,1)S(1)} %reshape.20, bf16[4096,501]{0,1:T(8,128)(2,1)} %param.7), kind=kOutput, calls=%fused_computation.21 | convolution fusion | flops 394050432 | bytes 5083392 | tf_op jit(solution)/shard_map/dot_general | solution.py:18
  58.0 36.9 %pmax.7 = f32[96]{0:T(128)S(1)} all-reduce(f32[96]{0:T(128)S(1)} %get-tuple-element.16), channel_id=1, replica_groups=mesh['tok'=8,'voc'=4] {'tok','voc'}, use_global_device_ids=true, to_apply=%region_3.4 | all-reduce | flops 96 | bytes 768 | tf_op jit(solution)/shard_map/pmax | solution.py:23
  94.9 0.2 dynamic-update-slice.2
  95.1 0.2 dynamic-update-slice
  95.4 41.1 %all-reduce.9 = (bf16[96]{0:T(256)(128)(2,1)S(1)}, bf16[96]{0:T(256)(128)(2,1)S(1)}) all-reduce(bf16[96]{0:T(256)(128)(2,1)S(1)} %dynamic-update-slice.2, bf16[96]{0:T(256)(128)(2,1)S(1)} %dynamic-update-slice), channel_id=1, replica_groups=mesh['tok'=8,'voc'=4] {'tok','voc'}, use_global_device_ids=true, to_apply=%add.2 | all-reduce | flops 192 | bytes 768
  136.5 0.2 dynamic-update-slice.1
  136.7 0.2 dynamic-update-slice.3
  137.0 39.5 %all-reduce.7 = (s32[96]{0:T(128)S(1)}, s32[96]{0:T(128)S(1)}) all-reduce(s32[96]{0:T(128)S(1)} %dynamic-update-slice.1, s32[96]{0:T(128)S(1)} %dynamic-update-slice.3), channel_id=1, replica_groups=mesh['tok'=8,'voc'=4] {'tok','voc'}, use_global_device_ids=true, to_apply=%add.1 | all-reduce | flops 192 | bytes 1536
  176.4 0.2 fusion.7
  176.7 40.5 %all-reduce.8 = (f32[96]{0:T(128)S(1)}, f32[96]{0:T(128)S(1)}, f32[96]{0:T(128)S(1)}) all-reduce(f32[96]{0:T(128)S(1)} %get-tuple-element.3, f32[96]{0:T(128)S(1)} %get-tuple-element.2, f32[96]{0:T(128)S(1)} %get-tuple-element.4), channel_id=1, replica_groups=mesh['tok'=8,'voc'=4] {'tok','voc'}, use_global_device_ids=true, to_apply=%region_7.8 | all-reduce | flops 288 | bytes 2304 | tf_op jit(solution)/shard_map/psum | solution.py:25
  217.2 3.2 fusion.9
  220.3 46.1 %fusion = f32[16,4096]{1,0:T(8,128)S(1)} fusion(f32[96,4096]{1,0:T(8,128)S(1)} %fusion.9), kind=kCustom, calls=%all-reduce-scatter | all-reduce-scatter fusion | flops 524289 | bytes 1835520
  266.5 4.3 %collective-permute-start = (f32[16,4096]{1,0:T(8,128)S(1)}, f32[16,4096]{1,0:T(8,128)S(1)}, u32[]{:S(2)}, u32[]{:S(2)}) collective-permute-start(f32[16,4096]{1,0:T(8,128)S(1)} %fusion), channel_id=1, source_target_pairs={{0,4},{4,8},{8,12},{12,16},{16,20},{20,24},{24,28},{1,5},{5,9},{9,... | collective-permute-start | bytes 786440
  270.8 2.7 collective-permute-start.1
  273.5 0.6 dynamic-slice.6
  274.7 2.6 collective-permute-done.1
  277.3 0.6 concatenate
  278.0 0.7 constant_dynamic-slice_fusion
  278.7 3.4 %fusion.1 = bf16[4096,501]{0,1:T(8,128)(2,1)} fusion(bf16[96,4096]{1,0:T(8,128)(2,1)S(1)} %reshape.20, f32[96,501]{1,0:T(8,128)S(1)} %get-tuple-element.17, f32[96]{0:T(128)S(1)} %get-tuple-element.14, f32[96]{0:T(128)S(1)} %get-tuple-element.15, f32[96]{0:T(128)S(1)} %get-tuple-element.13, f32[96]{0:T(128)S(1)} %get-tuple-element.12, ...), kind=kOutput, calls=%fused_computation.1 | convolution fusion | flops 396535488 | bytes 5086932 | tf_op jit(solution)/shard_map/dot_general | solution.py:51
  282.1 0.6 dynamic-slice.2
  283.4 31.4 %all-reduce.12.cloned.1.call-done = f32[12,4096]{1,0:T(8,128)} async-done(((f32[12,4096]{1,0:T(8,128)}), f32[12,4096]{1,0:T(8,128)}) %all-reduce.12.cloned.1.call-update) | async-done | bytes 196624
  314.7 1.6 constant_dynamic-slice_fusion.1
  (22 shorter events, 0.1 us)
Async XLA Ops:
  7.2 87.7 %copy-start.1 = (bf16[3]{0:T(256)(128)(2,1)S(1)}, bf16[3]{0:T(256)(128)(2,1)}, u32[]{:S(2)}) copy-start(bf16[3]{0:T(256)(128)(2,1)} %param.9) | copy-start | bytes 22
  7.2 88.0 %copy-start.2 = (bf16[3]{0:T(256)(128)(2,1)S(1)}, bf16[3]{0:T(256)(128)(2,1)}, u32[]{:S(2)}) copy-start(bf16[3]{0:T(256)(128)(2,1)} %param.10) | copy-start | bytes 22
  7.2 129.3 %copy-start.3 = (s32[3]{0:T(128)S(1)}, s32[3]{0:T(128)}, u32[]{:S(2)}) copy-start(s32[3]{0:T(128)} %param.8) | copy-start | bytes 40
  7.2 129.5 %copy-start.4 = (s32[3]{0:T(128)S(1)}, s32[3]{0:T(128)}, u32[]{:S(2)}) copy-start(s32[3]{0:T(128)} %param.11) | copy-start | bytes 40
  7.2 307.5 %all-reduce.12.cloned.1.call-start = ((), (), s32[]{:S(2)}) async-start(), calls=%async_computation | async-start | bytes 524288
  217.1 56.3 %copy-start = (u32[32]{0:T(128)S(1)}, u32[32]{0:T(128)}, u32[]{:S(2)}) copy-start(u32[32]{0:T(128)} %constant.50) | copy-start | bytes 388
  266.5 10.9 %collective-permute-start = (f32[16,4096]{1,0:T(8,128)S(1)}, f32[16,4096]{1,0:T(8,128)S(1)}, u32[]{:S(2)}, u32[]{:S(2)}) collective-permute-start(f32[16,4096]{1,0:T(8,128)S(1)} %fusion), channel_id=1, source_target_pairs={{0,4},{4,8},{8,12},{12,16},{16,20},{20,24},{24,28},{1,5},{5,9},{9,... | collective-permute-start | bytes 786440
  270.8 6.6 %collective-permute-start.1 = (f32[12,4096]{1,0:T(8,128)S(1)}, f32[12,4096]{1,0:T(8,128)S(1)}, u32[]{:S(2)}, u32[]{:S(2)}) collective-permute-start(f32[12,4096]{1,0:T(8,128)S(1)} %slice), channel_id=1, source_target_pairs={{0,8},{4,12},{8,16},{12,20},{16,24},{20,28},{1,9},{5,13},{9,17},{1... | collective-permute-start | bytes 589832
  278.0 4.1 %copy-start.5 = (u32[32]{0:T(128)S(1)}, u32[32]{0:T(128)}, u32[]{:S(2)}) copy-start(u32[32]{0:T(128)} %constant.54) | copy-start | bytes 388
Sparse Core Ops, SparseCore 0:
  278.9 35.7 all-reduce.11
where the time goes:
time: 324 us; the launch traced here: 323 us
  blocking collectives  250 us (77%)
  waiting for transfers between devices  34 us (10%)
  between operations  15.5 us (5%)
  matrix products  10.2 us (3%)
  starting transfers between devices  7 us (2%)
  local copies, waits for them, and re-layouts  5.77 us (2%)
    unnamed x3, blocking collectives  127 us
    all_gather x1, blocking collectives, per_device(): lax.all_gather(hidden, ('tok', 'voc'), axis=0, tiled=True)  46.5 us
    psum x1, blocking collectives, per_device(): lax.psum((jnp.sum(shifted, axis=1), jnp.sum(shifted * logits, axis=1), ta...  40.5 us
    pmax x1, blocking collectives, per_device(): top = lax.pmax(jnp.max(logits, axis=1), ('tok', 'voc'))  36.9 us
    unnamed x4, waiting for transfers between devices  34 us
    unnamed x3, starting transfers between devices  7 us
  transfers between devices with their start and end apart: 3, of which 2 were waited for; matrix products, arithmetic and copies ran while one was open for 1% of the time, Pallas kernels for 0%

commit v1 on v0

--- a/solution.py
+++ b/solution.py
@@ -23,7 +23,8 @@
     top = lax.pmax(jnp.max(logits, axis=1), ("tok", "voc"))
     shifted = jnp.exp(logits - top[:, None])
     sumexp, moment, target = lax.psum(
-        (jnp.sum(shifted, axis=1), jnp.sum(shifted * logits, axis=1), target_part), ("tok", "voc")
+        lax.psum((jnp.sum(shifted, axis=1), jnp.sum(shifted * logits, axis=1), target_part), "voc"),
+        "tok",
     )
     lse = top + jnp.log(sumexp)
     mean_logit = moment / sumexp

time: 324 us -> 301 us (0.929)
  blocking collectives: 250 us -> 230 us
    psum x1, blocking collectives: 40.5 us -> 5.83 us  [per_device(): lax.psum((jnp.sum(shifted, axis=1), jnp.sum(shifted * logits, axis=1), ta...]
    psum x0 -> x1, blocking collectives: none -> 20.4 us  [per_device(): lax.psum(lax.psum((jnp.sum(shifted, axis=1), jnp.sum(shifted * logits, ax...]
    unnamed x3, blocking collectives: 127 us -> 121 us
  transfers between devices with their start and end apart: 3 -> 3, of which waited for: 2 -> 2; matrix products, arithmetic and copies ran while one was open for 1% -> 2% of each run, Pallas kernels for 0% -> 0%
where the time goes in v1:
time: 301 us; the launch traced here: 300 us
  blocking collectives  230 us (76%)
  waiting for transfers between devices  31.6 us (10%)
  between operations  15.5 us (5%)
  matrix products  10.1 us (3%)
  starting transfers between devices  6.26 us (2%)
  local copies, waits for them, and re-layouts  5.76 us (2%)
    unnamed x3, blocking collectives  121 us
    all_gather x1, blocking collectives, per_device(): lax.all_gather(hidden, ('tok', 'voc'), axis=0, tiled=True)  46.5 us
    pmax x1, blocking collectives, per_device(): top = lax.pmax(jnp.max(logits, axis=1), ('tok', 'voc'))  36.8 us
    unnamed x4, waiting for transfers between devices  31.6 us
    psum x1, blocking collectives, per_device(): lax.psum(lax.psum((jnp.sum(shifted, axis=1), jnp.sum(shifted * logits, ax...  20.4 us
    unnamed x3, starting transfers between devices  6.26 us
  transfers between devices with their start and end apart: 3, of which 2 were waited for; matrix products, arithmetic and copies ran while one was open for 2% of the time, Pallas kernels for 0%

profile of v1, /device:TPU:0, one launch (start us, length us, event | category | flops | bytes accessed | tf_op | source)
XLA Modules:
  0.0 299.9 jit_solution(1283064194499250868)
XLA Ops:
  7.3 46.5 %all-gather = bf16[32,3,4096]{2,1,0:T(4,128)(2,1)S(1)} all-gather(bf16[1,3,4096]{2,1,0:T(4,128)(2,1)} %bitcast.11), channel_id=1, replica_groups=mesh['tok'=8,'voc'=4] {'tok','voc'}, dimensions={0}, use_global_device_ids=true | all-gather | bytes 811008 | tf_op jit(solution)/shard_map/all_gather | solution.py:9
  53.7 0.7 reshape.20
  54.4 3.6 %fusion.12 = (f32[96]{0:T(128)S(1)}, f32[96,501]{1,0:T(8,128)S(1)}) fusion(bf16[96,4096]{1,0:T(8,128)(2,1)S(1)} %reshape.20, bf16[4096,501]{0,1:T(8,128)(2,1)} %param.7), kind=kOutput, calls=%fused_computation.21 | convolution fusion | flops 394050432 | bytes 5083392 | tf_op jit(solution)/shard_map/dot_general | solution.py:18
  58.0 36.8 %pmax.7 = f32[96]{0:T(128)S(1)} all-reduce(f32[96]{0:T(128)S(1)} %get-tuple-element.19), channel_id=1, replica_groups=mesh['tok'=8,'voc'=4] {'tok','voc'}, use_global_device_ids=true, to_apply=%region_4.5 | all-reduce | flops 96 | bytes 768 | tf_op jit(solution)/shard_map/pmax | solution.py:23
  94.9 0.2 dynamic-update-slice.2
  95.1 0.2 dynamic-update-slice
  95.3 41.1 %all-reduce.10 = (bf16[96]{0:T(256)(128)(2,1)S(1)}, bf16[96]{0:T(256)(128)(2,1)S(1)}) all-reduce(bf16[96]{0:T(256)(128)(2,1)S(1)} %dynamic-update-slice.2, bf16[96]{0:T(256)(128)(2,1)S(1)} %dynamic-update-slice), channel_id=1, replica_groups=mesh['tok'=8,'voc'=4] {'tok','voc'}, use_global_device_ids=true, to_apply=%add.2 | all-reduce | flops 192 | bytes 768
  136.7 0.2 dynamic-update-slice.3
  136.9 39.5 %all-reduce.7 = (s32[96]{0:T(128)S(1)}, s32[96]{0:T(128)S(1)}) all-reduce(s32[96]{0:T(128)S(1)} %dynamic-update-slice.1, s32[96]{0:T(128)S(1)} %dynamic-update-slice.3), channel_id=1, replica_groups=mesh['tok'=8,'voc'=4] {'tok','voc'}, use_global_device_ids=true, to_apply=%add.1 | all-reduce | flops 192 | bytes 1536
  176.4 0.2 fusion.7
  176.6 5.8 %all-reduce.9 = (f32[96]{0:T(128)S(1)}, f32[96]{0:T(128)S(1)}, f32[96]{0:T(128)S(1)}) all-reduce(f32[96]{0:T(128)S(1)} %get-tuple-element.3, f32[96]{0:T(128)S(1)} %get-tuple-element.2, f32[96]{0:T(128)S(1)} %get-tuple-element.4), channel_id=1, replica_groups=mesh['tok'=8,'voc'=4] {'voc'}, use_global_device_ids=true, to_apply=%region_9.10 | all-reduce | flops 288 | bytes 2304 | tf_op jit(solution)/shard_map/psum | solution.py:26
  182.4 20.4 %all-reduce.8 = (f32[96]{0:T(128)S(1)}, f32[96]{0:T(128)S(1)}, f32[96]{0:T(128)S(1)}) all-reduce(f32[96]{0:T(128)S(1)} %get-tuple-element.10, f32[96]{0:T(128)S(1)} %get-tuple-element.11, f32[96]{0:T(128)S(1)} %get-tuple-element.12), channel_id=1, replica_groups=mesh['tok'=8,'voc'=4] {'tok'}, use_global_device_ids=true, to_apply=%region_10.11 | all-reduce | flops 288 | bytes 2304 | tf_op jit(solution)/shard_map/psum | solution.py:25
  202.9 3.2 %fusion.9 = f32[96,4096]{1,0:T(8,128)S(1)} fusion(bf16[4096,501]{0,1:T(8,128)(2,1)} %param.7, f32[96,501]{1,0:T(8,128)S(1)} %get-tuple-element.20, f32[96]{0:T(128)S(1)} %get-tuple-element.17, f32[96]{0:T(128)S(1)} %get-tuple-element.18, f32[96]{0:T(128)S(1)} %get-tuple-element.16, f32[96]{0:T(128)S(1)} %get-tuple-element.15, s32[501]{0:T(512)S(1)} %iota_add_fusion, ...), kind=kOutput, calls=%fused_computation.20 | convolution fusion | flops 394483392 | bytes 5873364 | tf_op jit(solution)/shard_map/dot_general | solution.py:44
  206.0 40.3 %fusion = f32[16,4096]{1,0:T(8,128)S(1)} fusion(f32[96,4096]{1,0:T(8,128)S(1)} %fusion.9), kind=kCustom, calls=%all-reduce-scatter | all-reduce-scatter fusion | flops 524289 | bytes 1835520
  246.4 2.8 collective-permute-start
  249.2 3.5 %collective-permute-start.1 = (f32[12,4096]{1,0:T(8,128)S(1)}, f32[12,4096]{1,0:T(8,128)S(1)}, u32[]{:S(2)}, u32[]{:S(2)}) collective-permute-start(f32[12,4096]{1,0:T(8,128)S(1)} %slice), channel_id=1, source_target_pairs={{0,8},{4,12},{8,16},{12,20},{16,24},{20,28},{1,9},{5,13},{9,17},{1... | collective-permute-start | bytes 589832
  252.6 0.6 dynamic-slice.6
  253.9 2.6 collective-permute-done.1
  256.5 0.6 concatenate
  257.1 0.7 constant_dynamic-slice_fusion
  257.9 3.4 %fusion.1 = bf16[4096,501]{0,1:T(8,128)(2,1)} fusion(bf16[96,4096]{1,0:T(8,128)(2,1)S(1)} %reshape.20, f32[96,501]{1,0:T(8,128)S(1)} %get-tuple-element.20, f32[96]{0:T(128)S(1)} %get-tuple-element.17, f32[96]{0:T(128)S(1)} %get-tuple-element.18, f32[96]{0:T(128)S(1)} %get-tuple-element.16, f32[96]{0:T(128)S(1)} %get-tuple-element.15, ...), kind=kOutput, calls=%fused_computation.1 | convolution fusion | flops 396535488 | bytes 5086932 | tf_op jit(solution)/shard_map/dot_general | solution.py:52
  261.3 0.6 dynamic-slice.2
  262.5 29.0 %all-reduce.13.cloned.1.call-done = f32[12,4096]{1,0:T(8,128)} async-done(((f32[12,4096]{1,0:T(8,128)}), f32[12,4096]{1,0:T(8,128)}) %all-reduce.13.cloned.1.call-update) | async-done | bytes 196624
  291.5 1.6 constant_dynamic-slice_fusion.1
  (23 shorter events, 0.4 us)
Async XLA Ops:
  7.2 87.7 %copy-start.1 = (bf16[3]{0:T(256)(128)(2,1)S(1)}, bf16[3]{0:T(256)(128)(2,1)}, u32[]{:S(2)}) copy-start(bf16[3]{0:T(256)(128)(2,1)} %param.9) | copy-start | bytes 22
  7.2 87.9 %copy-start.2 = (bf16[3]{0:T(256)(128)(2,1)S(1)}, bf16[3]{0:T(256)(128)(2,1)}, u32[]{:S(2)}) copy-start(bf16[3]{0:T(256)(128)(2,1)} %param.10) | copy-start | bytes 22
  7.2 129.3 %copy-start.3 = (s32[3]{0:T(128)S(1)}, s32[3]{0:T(128)}, u32[]{:S(2)}) copy-start(s32[3]{0:T(128)} %param.8) | copy-start | bytes 40
  7.2 129.5 %copy-start.4 = (s32[3]{0:T(128)S(1)}, s32[3]{0:T(128)}, u32[]{:S(2)}) copy-start(s32[3]{0:T(128)} %param.11) | copy-start | bytes 40
  7.2 284.3 %all-reduce.13.cloned.1.call-start = ((), (), s32[]{:S(2)}) async-start(), calls=%async_computation | async-start | bytes 524288
  202.9 49.8 %copy-start = (u32[32]{0:T(128)S(1)}, u32[32]{0:T(128)}, u32[]{:S(2)}) copy-start(u32[32]{0:T(128)} %constant.50) | copy-start | bytes 388
  246.4 10.1 %collective-permute-start = (f32[16,4096]{1,0:T(8,128)S(1)}, f32[16,4096]{1,0:T(8,128)S(1)}, u32[]{:S(2)}, u32[]{:S(2)}) collective-permute-start(f32[16,4096]{1,0:T(8,128)S(1)} %fusion), channel_id=1, source_target_pairs={{0,4},{4,8},{8,12},{12,16},{16,20},{20,24},{24,28},{1,5},{5,9},{9,... | collective-permute-start | bytes 786440
  249.2 7.3 %collective-permute-start.1 = (f32[12,4096]{1,0:T(8,128)S(1)}, f32[12,4096]{1,0:T(8,128)S(1)}, u32[]{:S(2)}, u32[]{:S(2)}) collective-permute-start(f32[12,4096]{1,0:T(8,128)S(1)} %slice), channel_id=1, source_target_pairs={{0,8},{4,12},{8,16},{12,20},{16,24},{20,28},{1,9},{5,13},{9,17},{1... | collective-permute-start | bytes 589832
  257.1 4.1 %copy-start.5 = (u32[32]{0:T(128)S(1)}, u32[32]{0:T(128)}, u32[]{:S(2)}) copy-start(u32[32]{0:T(128)} %constant.54) | copy-start | bytes 388
Sparse Core Ops, SparseCore 0:
  258.0 33.4 all-reduce.12
